TPU v7x, 32 devices: a whole 2x2x4 slice. The times are simulated.
32 devices in a mesh: blk: 8 (over y, x, core), width: 4 (over z).
Axes of the slice: x: 2, y: 2, z: 4, core: 2. Of those that a mesh axis runs over, the one named last changes fastest.
Arguments:
- inputs: bfloat16 [8, 128, 2048], P('blk', None, 'width'), may hold values from -6 to 6
- encoder: bfloat16 [8, 2048, 4096], P('blk', 'width'), may hold values from -0.125 to 0.125
- enc_bias: float32 [8, 4096], P('blk'), may hold values from -3 to 3
- active_blocks: int32 [8, 128, 32], P('blk'), may hold values 0 or 1
- near_decoders: bfloat16 [8, 4, 4096, 2048], P('blk', None, None, 'width'), may hold values from -0.09375 to 0.09375
- far_decoders: bfloat16 [8, 2048, 2048], P('blk', None, 'width'), may hold values from -0.09375 to 0.09375
- targets: bfloat16 [8, 128, 2048], P('blk', None, 'width'), may hold values from -6 to 6
Outputs:
- reconstruction: float32 [8, 128, 2048], P('blk', None, 'width')
- grad_encoder: bfloat16 [8, 2048, 4096], P('blk', 'width')
- grad_bias: float32 [8, 4096], P('blk')
All inputs are finite; a program needn't handle non-finite values. No bound on the sum of `active_blocks` on one device may be relied on, other than what follows from the above.
Results may differ from a plain program's by a relative error of at most 0.011.
Values may be sent and summed in bfloat16 or wider, within the bound.
A program may use at most 128 MiB of HBM per device.

v0:
```python
import functools

import jax
import jax.numpy as jnp
from jax import lax
from jax.experimental import pallas as pl
from jax.experimental.pallas import tpu as pltpu
from jax.sharding import PartitionSpec as P

BF = jnp.bfloat16
F32 = jnp.float32


def dot(a, b):
    return jnp.dot(a, b, preferred_element_type=F32)


def dot_t(a, b):
    return lax.dot_general(a, b, (((1,), (1,)), ((), ())), preferred_element_type=F32)


def step_kernel(B, W, C, FBLK, x_ref, enc_hbm, bias_ref, blocks_ref, near_hbm, far_hbm, tgt_ref,
                recon_ref, pg_ref,
                enc, near, far, z1_out, z1_in, acts, p_out, p_in, og, terms, duo, ret, own, z3_out, z3_in, pg,
                enc_sem, near_sem, far_sem, z1_s, z1_r, z2_s, z2_r, ad_s, af_s, a_r, p_s, p_r, o_s, o_r,
                d_s, d_r, r_s, r_r, z3_s, z3_r, z4_s, z4_r):
    N = B // 2
    H = W // 2
    b = lax.axis_index("blk")
    w = lax.axis_index("width")
    even = lax.rem(b, 2) == 0
    odd = lax.rem(b, 2) == 1
    relay = N == 4
    mid = (b >= N - 2) & (b < N) & relay
    top = (b >= B - 2) & relay
    not_mid = jnp.logical_not(mid)
    not_top = jnp.logical_not(top)

    def col(j):
        return pl.ds(pl.multiple_of(j * C, C), C)

    def blk(d):
        return lax.rem(w + d, W)

    def remote(src, dst, s, r, to_b, to_w):
        return pltpu.make_async_remote_copy(src_ref=src, dst_ref=dst, send_sem=s, recv_sem=r,
                                            device_id=(to_b, to_w), device_id_type=pl.DeviceIdType.MESH)

    def loop(lo, hi, body):
        def run(i, carry):
            body(i)
            return carry
        lax.fori_loop(lo, hi, run, 0)

    def enc_copy(j):
        return pltpu.make_async_copy(enc_hbm.at[:, col(j)], enc.at[:, col(j)], enc_sem.at[j])

    def near_copy(k):
        return pltpu.make_async_copy(near_hbm.at[k], near.at[k], near_sem.at[k])

    far_copy = pltpu.make_async_copy(far_hbm, far, far_sem)

    def z1(j):
        return remote(z1_out.at[j], z1_in.at[w], z1_s.at[j], z1_r.at[w], b, j)

    def z1_arrival(j):
        return remote(z1_out.at[j], z1_in.at[j], z1_s.at[j], z1_r.at[j], b, j)

    def z2(j):
        return remote(acts.at[0, w], acts.at[0, w], z2_s.at[j], z2_r.at[w], b, j)

    def z2_arrival(j):
        return remote(acts.at[0, j], acts.at[0, j], z2_s.at[j], z2_r.at[j], b, j)

    def z3(j):
        return remote(z3_out.at[j], z3_in.at[w], z3_s.at[j], z3_r.at[w], b, j)

    def z3_arrival(j):
        return remote(z3_out.at[j], z3_in.at[j], z3_s.at[j], z3_r.at[j], b, j)

    def z4(j):
        return remote(pg.at[w], pg.at[w], z4_s.at[j], z4_r.at[w], b, j)

    def z4_arrival(j):
        return remote(pg.at[j], pg.at[j], z4_s.at[j], z4_r.at[j], b, j)

    def act_direct(k, j):
        return remote(acts.at[0, j], acts.at[k, j], ad_s.at[k, j], a_r.at[k, j], b + k, w)

    def act_pass(k_from, k, j, to):
        return remote(acts.at[k_from, j], acts.at[k, j], af_s.at[k, j], a_r.at[k, j], to, w)

    def share(k):
        return remote(p_out.at[k], p_in.at[k], p_s.at[k], p_r.at[k], b - k + B, w)

    def out_grad(k):
        return remote(og.at[0], og.at[k], o_s.at[k], o_r.at[k], b + k - B, w)

    def duo_copy(k_from, k, j, to):
        return remote(terms.at[k_from, j], duo.at[k, j], d_s.at[k_from, j], d_r.at[k, j], to, w)

    def ret_copy(k, j, to):
        return remote(terms.at[k, j], ret.at[k, j], r_s.at[k, j], r_r.at[k, j], to, w)

    loop(1, W + 1, lambda d: enc_copy(blk(d)).start())
    for k in range(N):
        near_copy(k).start()
    far_copy.start()

    barrier = pltpu.get_barrier_semaphore()
    for d in range(1, W):
        pl.semaphore_signal(barrier, inc=1, device_id=(b, lax.rem(w + d, W)), device_id_type=pl.DeviceIdType.MESH)
    for d in range(1, B):
        pl.semaphore_signal(barrier, inc=1, device_id=(lax.rem(b + d, B), w), device_id_type=pl.DeviceIdType.MESH)
    pl.semaphore_wait(barrier, W + B - 2)

    def first(d):
        j = blk(d)
        enc_copy(j).wait()
        z1_out[j] = dot(x_ref[...], enc[:, col(j)]).astype(BF)
        z1(j).start()

    loop(1, W, first)
    enc_copy(w).wait()
    own[w] = dot(x_ref[...], enc[:, col(w)]) + bias_ref[:, col(w)]
    fb = blocks_ref.shape[1]
    row_id = lax.broadcasted_iota(jnp.int32, (fb, C), 0) - w * (C // FBLK)
    lane_id = lax.broadcasted_iota(jnp.int32, (fb, C), 1) // FBLK
    spread = jnp.where(row_id == lane_id, 1.0, 0.0).astype(BF)

    def mask():
        return dot(blocks_ref[...].astype(F32).astype(BF), spread)

    def gather1(d):
        j = blk(d)
        z1_arrival(j).wait_recv()
        own[w] += z1_in[j].astype(F32)

    loop(1, W, gather1)
    acts[0, w] = (mask() * own[w]).astype(BF)
    loop(1, W, lambda d: z2(blk(d)).start())

    def act_sends(j, act):
        for k in range(2, N, 2):
            @pl.when((b + k < B) & not_mid)
            def _():
                act(act_direct(k, j))

        @pl.when(even)
        def _():
            act(act_pass(0, 1, j, b + 1))

        @pl.when(odd & (b + N - 1 < B) & not_mid)
        def _():
            act(act_direct(N - 1, j))

        @pl.when(mid | (even & (b + N < B) & (j >= H)))
        def _():
            act(act_direct(N, j))

    start = lambda c: c.start()
    end = lambda c: c.wait_send()
    act_sends(w, start)

    def gather2(d):
        j = blk(d)
        z2_arrival(j).wait_recv()
        act_sends(j, start)

    loop(1, W, gather2)
    for k in range(N):
        near_copy(k).wait()
    far_copy.wait()

    def own_term(k):
        def body(j):
            recon_ref[...] += dot(acts[0, j], near[k, col(j), :])
        return body

    def far_term(j):
        recon_ref[...] += dot(acts[0, j], far[col(j), :])

    for k in range(1, N + 1):
        @pl.when(b < k)
        def _():
            recon_ref[...] = jnp.zeros(recon_ref.shape, F32)
            if k < N:
                loop(0, W, own_term(k))
            else:
                loop(0, H, far_term)
            p_out[k] = recon_ref[...].astype(BF)
            share(k).start()

    recon_ref[...] = jnp.zeros(recon_ref.shape, F32)
    loop(0, W, own_term(0))

    def inside_term(k, j):
        if k < N:
            recon_ref[...] += dot(acts[k, j], near[k, col(j), :])
        else:
            recon_ref[...] += dot(acts[k, j], far[col(j - H), :])

    def act_forwards(k, j, act):
        if k % 2 == 0 and k < N:
            @pl.when(even)
            def _():
                act(act_pass(k, k + 1, j, b + 1))

            @pl.when(odd)
            def _():
                act(act_pass(k, k - 1, j, b - 1))
        if k == N - 1:
            @pl.when(j >= H)
            def _():
                act(act_pass(k, N, j, b + 1))

    def arrival(k, j):
        return remote(acts.at[k, j], acts.at[k, j], ad_s.at[k, j], a_r.at[k, j], b, w)

    def relay_sends(j, act):
        act(act_pass(N, 2, j, b - 2))

        @pl.when(odd)
        def _():
            act(act_pass(N, N - 1, j, b - 1))

    def inner(d):
        j = blk(d)
        if relay:
            @pl.when(top)
            def _():
                arrival(N, j).wait_recv()
                relay_sends(j, start)

                @pl.when(j >= H)
                def _():
                    inside_term(N, j)
        for k in list(range(2, N, 2)) + [N - 1, N]:
            cond = b >= k
            if k >= N - 1:
                cond = cond & even & not_top
            if k == N:
                cond = cond & (j >= H)

            @pl.when(cond)
            def _():
                arrival(k, j).wait_recv()
                act_forwards(k, j, start)
                inside_term(k, j)

    loop(0, W, inner)

    def passed(d):
        j = blk(d)
        for k in list(range(1, N, 2)) + [N]:
            cond = b >= k
            if k == N - 1:
                cond = cond & (odd | top)
            if k == N:
                cond = cond & odd & not_top
            if k == N:
                cond = cond & (j >= H)

            @pl.when(cond)
            def _():
                arrival(k, j).wait_recv()
                inside_term(k, j)

    loop(0, W, passed)
    for k in range(1, N + 1):
        @pl.when(b + k >= B)
        def _():
            remote(p_out.at[k], p_in.at[k], p_s.at[k], p_r.at[k], b, w).wait_recv()
            recon_ref[...] += p_in[k].astype(F32)

    og[0] = (recon_ref[...] - tgt_ref[...].astype(F32)).astype(BF)
    for k in range(1, N + 1):
        @pl.when(b + k >= B)
        def _():
            out_grad(k).start()

    def back(d):
        j = blk(d)
        for k in list(range(1, N, 2)) + [N] + list(range(2, N, 2)):
            cond = b >= k
            if k == N:
                cond = cond & (j >= H)

            @pl.when(cond)
            def _():
                rows = near[k, col(j), :] if k < N else far[col(j - H), :]
                terms[k, j] = dot_t(og[0], rows).astype(BF)
                duo_sends(k, j, start)

    def duo_sends(k, j, act):
        if k % 2 == 1 and k <= N - 3:
            @pl.when(even)
            def _():
                act(duo_copy(k, k + 1, j, b + 1))
        if k == 1:
            @pl.when(odd)
            def _():
                act(ret_copy(1, j, b - 1))
        if k % 2 == 1 and k >= 3:
            @pl.when(odd)
            def _():
                act(duo_copy(k, k - 1, j, b - 1))
        if k == N:
            @pl.when(odd)
            def _():
                act(duo_copy(N, N - 1, j, b - 1))

            @pl.when(even)
            def _():
                act(ret_copy(N, j, b - N))

    loop(1, W + 1, back)

    def duo_add(k, j):
        remote(duo.at[k, j], duo.at[k, j], d_s.at[k, j], d_r.at[k, j], b, w).wait_recv()
        terms[k, j] = (terms[k, j].astype(F32) + duo[k, j].astype(F32)).astype(BF)

    def down(d):
        j = blk(d)
        for k in range(2, N, 2):
            @pl.when(b >= k)
            def _():
                duo_add(k, j)
                ret_copy(k, j, b - k).start()

        @pl.when(even & (b >= N - 1))
        def _():
            @pl.when(j >= H)
            def _():
                duo_add(N - 1, j)
            ret_copy(N - 1, j, b - (N - 1)).start()

    loop(1, W + 1, down)

    for k in range(1, N + 1):
        @pl.when(b < k)
        def _():
            remote(og.at[k], og.at[k], o_s.at[k], o_r.at[k], b, w).wait_recv()

    def own_back(j):
        own[j] = dot_t(og[0], near[0, col(j), :])
        for k in range(1, N):
            @pl.when(b < k)
            def _():
                own[j] += dot_t(og[k], near[k, col(j), :])

        @pl.when((b < N) & (j < H))
        def _():
            own[j] += dot_t(og[N], far[col(j), :])

    loop(0, W, own_back)

    def ret_add(k, j):
        remote(ret.at[k, j], ret.at[k, j], r_s.at[k, j], r_r.at[k, j], b, w).wait_recv()
        own[j] += ret[k, j].astype(F32)

    def collect(j):
        @pl.when(even)
        def _():
            ret_add(1, j)
        for k in range(2, N, 2):
            @pl.when(b + k < B)
            def _():
                ret_add(k, j)

        @pl.when(odd & (b + N - 1 < B))
        def _():
            ret_add(N - 1, j)

        @pl.when(even & (b + N < B) & (j >= H))
        def _():
            ret_add(N, j)

    def third(d):
        j = blk(d)
        collect(j)
        z3_out[j] = own[j].astype(BF)
        z3(j).start()

    loop(1, W, third)
    collect(w)

    def gather3(d):
        j = blk(d)
        z3_arrival(j).wait_recv()
        own[w] += z3_in[j].astype(F32)

    loop(1, W, gather3)
    pg[w] = (mask() * own[w]).astype(BF)
    loop(1, W, lambda d: z4(blk(d)).start())
    pg_ref[:, col(w)] = pg[w]

    def gather4(d):
        j = blk(d)
        z4_arrival(j).wait_recv()
        pg_ref[:, col(j)] = pg[j]

    loop(1, W, gather4)

    def drain(d):
        j = blk(d)
        z1(j).wait_send()
        z2(j).wait_send()
        z3(j).wait_send()
        z4(j).wait_send()

    loop(1, W, drain)

    def drain_blk(j):
        act_sends(j, end)
        for k in list(range(2, N, 2)) + [N - 1]:
            cond = b >= k
            if k == N - 1:
                cond = cond & even & not_top

            @pl.when(cond)
            def _():
                act_forwards(k, j, end)
        if relay:
            @pl.when(top)
            def _():
                relay_sends(j, end)
        for k in range(1, N + 1):
            cond = b >= k
            if k == N:
                cond = cond & (j >= H)

            @pl.when(cond)
            def _():
                duo_sends(k, j, end)
        for k in range(2, N, 2):
            @pl.when(b >= k)
            def _():
                ret_copy(k, j, b - k).wait_send()

        @pl.when(even & (b >= N - 1))
        def _():
            ret_copy(N - 1, j, b - (N - 1)).wait_send()

    loop(0, W, drain_blk)
    for k in range(1, N + 1):
        @pl.when(b < k)
        def _():
            share(k).wait_send()

        @pl.when(b + k >= B)
        def _():
            out_grad(k).wait_send()


def weight_kernel(x_ref, pg_ref, grad_ref, bias_ref):
    grads = pg_ref[...]
    grad_ref[...] = lax.dot_general(
        x_ref[...], grads, (((0,), (0,)), ((), ())), preferred_element_type=F32
    ).astype(BF)
    bias_ref[...] = jnp.sum(grads.astype(F32), axis=0, keepdims=True)


def on_device(B, W, inputs, encoder, enc_bias, active_blocks, near_decoders, far_decoders, targets):
    N = B // 2
    x = inputs[0]
    tok, width = x.shape
    feats = encoder.shape[2]
    half = far_decoders.shape[1]
    out_cols = targets.shape[2]
    C = feats // W
    dma = pltpu.SemaphoreType.DMA
    blocks = lambda *lead: pltpu.VMEM((*lead, tok, C), BF)
    rows = lambda *lead: pltpu.VMEM((*lead, tok, out_cols), BF)
    vmem = pl.BlockSpec(memory_space=pltpu.VMEM)
    hbm = pl.BlockSpec(memory_space=pl.ANY)
    recon, pre_grad = pl.pallas_call(
        functools.partial(step_kernel, B, W, C, feats // active_blocks.shape[2]),
        out_shape=(jax.ShapeDtypeStruct((tok, out_cols), F32), jax.ShapeDtypeStruct((tok, feats), BF)),
        in_specs=[vmem, hbm, vmem, vmem, hbm, hbm, vmem],
        out_specs=(vmem, vmem),
        scratch_shapes=[
            pltpu.VMEM((width, feats), BF),
            pltpu.VMEM((N, feats, out_cols), BF),
            pltpu.VMEM((half, out_cols), BF),
            blocks(W), blocks(W), blocks(N + 1, W),
            rows(N + 1), rows(N + 1), rows(N + 1),
            blocks(N + 1, W), blocks(N, W), blocks(N + 1, W),
            pltpu.VMEM((W, tok, C), F32),
            blocks(W), blocks(W), blocks(W),
            dma((W,)), dma((N,)), dma,
            dma((W,)), dma((W,)), dma((W,)), dma((W,)),
            dma((N + 1, W)), dma((N + 1, W)), dma((N + 1, W)),
            dma((N + 1,)), dma((N + 1,)), dma((N + 1,)), dma((N + 1,)),
            dma((N + 1, W)), dma((N, W)), dma((N + 1, W)), dma((N + 1, W)),
            dma((W,)), dma((W,)), dma((W,)), dma((W,)),
        ],
        compiler_params=pltpu.CompilerParams(
            collective_id=0, has_side_effects=True, vmem_limit_bytes=67_000_000),
        name="step",
    )(x, encoder[0], enc_bias, active_blocks[0], near_decoders[0], far_decoders[0], targets[0])
    tile = min(feats, 1024)
    enc_grad, bias_grad = pl.pallas_call(
        weight_kernel,
        grid=(feats // tile,),
        out_shape=(jax.ShapeDtypeStruct((width, feats), BF), jax.ShapeDtypeStruct((1, feats), F32)),
        in_specs=[pl.BlockSpec((tok, width), lambda i: (0, 0)), pl.BlockSpec((tok, tile), lambda i: (0, i))],
        out_specs=(pl.BlockSpec((width, tile), lambda i: (0, i)), pl.BlockSpec((1, tile), lambda i: (0, i))),
        name="weights",
    )(x, pre_grad)
    return recon[None], enc_grad[None], bias_grad


def solution(mesh):
    return jax.shard_map(
        functools.partial(on_device, mesh.shape["blk"], mesh.shape["width"]),
        mesh=mesh,
        in_specs=(
            P("blk", None, "width"),
            P("blk", "width", None),
            P("blk", None),
            P("blk", None, None),
            P("blk", None, None, "width"),
            P("blk", None, "width"),
            P("blk", None, "width"),
        ),
        out_specs=(P("blk", None, "width"), P("blk", "width", None), P("blk", None)),
        check_vma=False,
    )
```

profile of v0, /device:TPU:16, one launch (start us, length us, event | category | flops | bytes accessed | tf_op | source)
XLA Modules:
  0.0 164.8 jit_solution(10106720882214918251)
XLA Ops:
  0.6 1.4 copy.10
  2.1 156.2 %step.1 = (f32[128,512]{1,0:T(8,128)}, bf16[128,4096]{1,0:T(8,128)(2,1)}) custom-call(bf16[128,512]{1,0:T(8,128)(2,1)} %bitcast.11, bf16[512,4096]{1,0:T(8,128)(2,1)} %bitcast.9, f32[1,4096]{1,0:T(1,128)} %bias_ref.1, s32[128,32]{1,0:T(8,128)} %bitcast.13, bf16[4,4096,512]{2,1,0:T(8,128)(2,1)} %bitcast.8, bf16[2048,512]{1,0:T(8,128)(2,1)} %bitcast.10, ...), custom_call_target="tpu_custom_call" | custom-call | tf_op jit(solution)/shard_map/step/pallas_call | solution.py:477
  158.3 4.8 %weights.1 = (bf16[512,4096]{1,0:T(8,128)(2,1)}, f32[1,4096]{1,0:T(1,128)}) custom-call(bf16[128,512]{1,0:T(8,128)(2,1)} %bitcast.12, bf16[128,4096]{1,0:T(8,128)(2,1)} %get-tuple-element.8.pg_ref), custom_call_target="tpu_custom_call" | custom-call | tf_op jit(solution)/shard_map/weights/pallas_call | solution.py:503
  163.1 1.7 %copy.12 = f32[1,128,512]{2,1,0:T(8,128)} copy(f32[1,128,512]{2,1,0:T(8,128)} %bitcast.14) | data formatting | bytes 524288
where the time goes:
time: 165 us
  Pallas kernels  161 us (98%)
  local copies, waits for them, and re-layouts  3.12 us (2%)
    pallas_call x1, Pallas kernels, on_device(): pl.pallas_call(functools.partial(step_kernel, B, W, C, feats // active_bl...  156 us
    pallas_call x1, Pallas kernels, on_device(): pl.pallas_call(weight_kernel, grid=(feats // tile,), out_shape=(jax.Shape...  4.83 us

commit v1 on v0

v1 whole, which is shorter than its diff:
```python
import functools

import jax
import jax.numpy as jnp
from jax import lax
from jax.experimental import pallas as pl
from jax.experimental.pallas import tpu as pltpu
from jax.sharding import PartitionSpec as P

BF = jnp.bfloat16
F32 = jnp.float32


def dot(a, b):
    return jnp.dot(a, b, preferred_element_type=F32)


def dot_t(a, b):
    return lax.dot_general(a, b, (((1,), (1,)), ((), ())), preferred_element_type=F32)


def step_kernel(B, W, C, FBLK, x_ref, enc_hbm, bias_ref, blocks_ref, near_hbm, far_hbm, tgt_ref,
                recon_ref, pg_ref, gb_ref,
                enc, near, far, z_out, z_in, acts, p_acc, p_out, p_in, og, terms, duo, ret, rel, own, mask, gb,
                enc_sem, near_sem, far_sem, z_s, z_r, ad_s, af_s, a_r, p_s, p_r, o_s, o_r,
                d_s, d_r, r_s, r_r, l_s, l_r, g_s, g_r):
    N = B // 2
    G = mask.shape[0]
    H = G // 2
    ROOT = W // 2
    b = lax.axis_index("blk")
    w = lax.axis_index("width")
    even = lax.rem(b, 2) == 0
    odd = lax.rem(b, 2) == 1
    relay = N == 4
    mid = (b >= N - 2) & (b < N) & relay
    top = (b >= B - 2) & relay
    far_side = (b >= N) & (b < B - 2) & relay
    not_mid = jnp.logical_not(mid)
    not_top = jnp.logical_not(top)
    not_far_side = jnp.logical_not(far_side)
    chip = lax.div(b, 2)
    late = 2 * (lax.div(chip, 2) - lax.div(chip, 3)) if relay else 0

    def col(j):
        return pl.ds(pl.multiple_of(j * C, C), C)

    def remote(src, dst, s, r, to_b, to_w):
        return pltpu.make_async_remote_copy(src_ref=src, dst_ref=dst, send_sem=s, recv_sem=r,
                                            device_id=(to_b, to_w), device_id_type=pl.DeviceIdType.MESH)

    def loop(lo, hi, body):
        def run(i, carry):
            body(i)
            return carry
        lax.fori_loop(lo, hi, run, 0)

    def inside(j):
        return (j >= 0) & (j < G)

    def enc_copy(j):
        return pltpu.make_async_copy(enc_hbm.at[:, col(j)], enc.at[:, col(j)], enc_sem.at[j])

    def near_copy(k):
        return pltpu.make_async_copy(near_hbm.at[k], near.at[k], near_sem.at[k])

    far_copy = pltpu.make_async_copy(far_hbm, far, far_sem)

    def z_copy(lane, j, to):
        return remote(z_out.at[lane, j], z_in.at[lane, j], z_s.at[lane, j], z_r.at[lane, j], b, to)

    def act_direct(k, j):
        return remote(acts.at[0, j], acts.at[k, j], ad_s.at[k, j], a_r.at[k, j], b + k, w)

    def act_pass(k_from, k, j, to):
        return remote(acts.at[k_from, j], acts.at[k, j], af_s.at[k, j], a_r.at[k, j], to, w)

    def share(k):
        return remote(p_out.at[k], p_in.at[k], p_s.at[k], p_r.at[k], b - k + B, w)

    def out_grad(k):
        return remote(og.at[0], og.at[k], o_s.at[k], o_r.at[k], b + k - B, w)

    def duo_copy(k_from, k, j, to):
        return remote(terms.at[k_from, j], duo.at[k, j], d_s.at[k_from, j], d_r.at[k, j], to, w)

    def ret_copy(k_from, k, j, to):
        return remote(terms.at[k_from, j], ret.at[k, j], r_s.at[k_from, j], r_r.at[k, j], to, w)

    def rel_copy(j):
        return remote(terms.at[2, j], rel.at[j], l_s.at[j], l_r.at[j], b + 2, w)

    def bias_copy(d):
        return remote(gb, gb, g_s.at[d], g_r, b, lax.rem(w + d, W))

    loop(0, G, lambda j: enc_copy(j).start())

    barrier = pltpu.get_barrier_semaphore()
    for d in range(1, W):
        pl.semaphore_signal(barrier, inc=1, device_id=(b, lax.rem(w + d, W)), device_id_type=pl.DeviceIdType.MESH)
    for d in range(1, B):
        pl.semaphore_signal(barrier, inc=1, device_id=(lax.rem(b + d, B), w), device_id_type=pl.DeviceIdType.MESH)

    fb = blocks_ref.shape[0]
    active = blocks_ref[...].astype(F32).astype(BF)
    row_id = lax.broadcasted_iota(jnp.int32, (fb, C), 0)
    lane_id = lax.broadcasted_iota(jnp.int32, (fb, C), 1) // FBLK

    def masks(j):
        spread = jnp.where(row_id - j * (C // FBLK) == lane_id, 1.0, 0.0).astype(BF)
        mask[j] = lax.dot_general(active, spread, (((0,), (0,)), ((), ())), preferred_element_type=F32).astype(BF)

    loop(0, G, masks)
    recon_ref[...] = jnp.zeros(recon_ref.shape, F32)
    p_acc[...] = jnp.zeros(p_acc.shape, F32)
    pl.semaphore_wait(barrier, W + B - 2)

    def ends(phase, j):
        @pl.when(w == 0)
        def _():
            z_out[2 * phase, j] = own[j].astype(BF)
            z_copy(2 * phase, j, w + 1).start()

        @pl.when(w == W - 1)
        def _():
            z_out[2 * phase + 1, j] = own[j].astype(BF)
            z_copy(2 * phase + 1, j, w - 1).start()

    def first(j):
        enc_copy(j).wait()
        own[j] = dot(x_ref[...], enc[:, col(j)])
        ends(0, j)

    loop(0, G, first)
    for k in range(N):
        near_copy(k).start()
    far_copy.start()

    def hop(phase, t):
        up = t - w + 1
        down = t - (W - 2) + w

        @pl.when((w > 0) & inside(up))
        def _():
            z_copy(2 * phase, up, w).wait_recv()

            @pl.when(w < W - 1)
            def _():
                z_out[2 * phase, up] = (own[up] + z_in[2 * phase, up].astype(F32)).astype(BF)
                z_copy(2 * phase, up, w + 1).start()

        @pl.when((w < W - 1) & inside(down))
        def _():
            z_copy(2 * phase + 1, down, w).wait_recv()

            @pl.when(w > 0)
            def _():
                z_out[2 * phase + 1, down] = (own[down] + z_in[2 * phase + 1, down].astype(F32)).astype(BF)
                z_copy(2 * phase + 1, down, w - 1).start()

    def total(phase, j, put):
        @pl.when(w == 0)
        def _():
            put(own[j] + z_in[2 * phase + 1, j].astype(F32))

        @pl.when(w == W - 1)
        def _():
            put(own[j] + z_in[2 * phase, j].astype(F32))

        @pl.when((w > 0) & (w < W - 1))
        def _():
            put(own[j] + z_in[2 * phase, j].astype(F32) + z_in[2 * phase + 1, j].astype(F32))

    def act_sends(j, act):
        for k in range(2, N, 2):
            @pl.when((b + k < B) & not_mid)
            def _():
                act(act_direct(k, j))

        @pl.when(even)
        def _():
            act(act_pass(0, 1, j, b + 1))

        @pl.when(odd & (b + N - 1 < B) & not_mid)
        def _():
            act(act_direct(N - 1, j))

        @pl.when(mid | (even & (b + N < B) & (j >= H)))
        def _():
            act(act_direct(N, j))

    start = lambda c: c.start()
    end = lambda c: c.wait_send()

    def finish(j):
        def put(value):
            acts[0, j] = (mask[j].astype(F32) * (value + bias_ref[:, col(j)])).astype(BF)

        total(0, j, put)
        act_sends(j, start)
        recon_ref[...] += dot(acts[0, j], near[0, col(j), :])
        for k in range(1, N):
            @pl.when(b < k)
            def _():
                p_acc[k] += dot(acts[0, j], near[k, col(j), :])

        @pl.when((b < N) & (j < H))
        def _():
            p_acc[N] += dot(acts[0, j], far[col(j), :])

    def inside_term(k, j):
        if k < N:
            recon_ref[...] += dot(acts[k, j], near[k, col(j), :])
        else:
            recon_ref[...] += dot(acts[k, j], far[col(j - H), :])

    def act_forwards(k, j, act):
        if k % 2 == 0 and k < N:
            @pl.when(even)
            def _():
                act(act_pass(k, k + 1, j, b + 1))

            @pl.when(odd)
            def _():
                act(act_pass(k, k - 1, j, b - 1))
        if k == N - 1:
            @pl.when(j >= H)
            def _():
                act(act_pass(k, N, j, b + 1))

    def arrival(k, j):
        return remote(acts.at[k, j], acts.at[k, j], ad_s.at[k, j], a_r.at[k, j], b, w)

    def relay_sends(j, act):
        act(act_pass(N, 2, j, b - 2))

        @pl.when(odd)
        def _():
            act(act_pass(N, N - 1, j, b - 1))

    def inner(j):
        if relay:
            @pl.when(top)
            def _():
                arrival(N, j).wait_recv()
                relay_sends(j, start)

                @pl.when(j >= H)
                def _():
                    inside_term(N, j)
        for k in list(range(2, N, 2)) + [N - 1, N]:
            cond = b >= k
            if k >= N - 1:
                cond = cond & even & not_top
            if k == N:
                cond = cond & (j >= H)

            @pl.when(cond)
            def _():
                arrival(k, j).wait_recv()
                act_forwards(k, j, start)
                inside_term(k, j)

    def passed(j):
        for k in list(range(1, N, 2)) + [N]:
            cond = b >= k
            if k == N - 1:
                cond = cond & (odd | top)
            if k == N:
                cond = cond & odd & not_top
            if k == N:
                cond = cond & (j >= H)

            @pl.when(cond)
            def _():
                arrival(k, j).wait_recv()
                inside_term(k, j)

    AHEAD, BEHIND = 3, 3

    def forward(t):
        hop(0, t)
        f = t - (W - 2)

        @pl.when(f == 0)
        def _():
            for k in range(N):
                near_copy(k).wait()
            far_copy.wait()

        @pl.when(inside(f))
        def _():
            finish(f)

        for k in range(1, N + 1):
            @pl.when((f == G - 1) & (b < k))
            def _():
                p_out[k] = p_acc[k].astype(BF)
                share(k).start()

        i = f - AHEAD - late

        @pl.when(inside(i))
        def _():
            inner(i)

        p = i - BEHIND

        @pl.when(inside(p))
        def _():
            passed(p)

    loop(0, G + W - 2 + AHEAD + BEHIND + (2 if relay else 0), forward)
    for k in range(1, N + 1):
        @pl.when(b + k >= B)
        def _():
            remote(p_out.at[k], p_in.at[k], p_s.at[k], p_r.at[k], b, w).wait_recv()
            recon_ref[...] += p_in[k].astype(F32)

    og[0] = (recon_ref[...] - tgt_ref[...].astype(F32)).astype(BF)
    for k in range(1, N + 1):
        @pl.when(b + k >= B)
        def _():
            out_grad(k).start()

    def back(j):
        for k in list(range(1, N, 2)) + [N] + list(range(2, N, 2)):
            cond = b >= k
            if k == N:
                cond = cond & (j >= H)

            @pl.when(cond)
            def _():
                rows = near[k, col(j), :] if k < N else far[col(j - H), :]
                terms[k, j] = dot_t(og[0], rows).astype(BF)
                duo_sends(k, j, start)

    def duo_sends(k, j, act):
        if k % 2 == 1 and k <= N - 3:
            @pl.when(even)
            def _():
                act(duo_copy(k, k + 1, j, b + 1))
        if k == 1:
            @pl.when(odd)
            def _():
                act(ret_copy(1, 1, j, b - 1))
        if k % 2 == 1 and k >= 3:
            @pl.when(odd)
            def _():
                act(duo_copy(k, k - 1, j, b - 1))
        if k == N - 1 and relay:
            @pl.when(even & top)
            def _():
                act(duo_copy(k, k, j, b + 1))
        if k == N:
            @pl.when(odd & not_top)
            def _():
                act(duo_copy(N, N - 1, j, b - 1))

            @pl.when(even & not_top)
            def _():
                act(ret_copy(N, N, j, b - N))

    def duo_wait(k, j):
        remote(duo.at[k, j], duo.at[k, j], d_s.at[k, j], d_r.at[k, j], b, w).wait_recv()

    def duo_add(k, j):
        duo_wait(k, j)
        terms[k, j] = (terms[k, j].astype(F32) + duo[k, j].astype(F32)).astype(BF)

    def down_sends(k, j, act):
        @pl.when(not_far_side)
        def _():
            act(ret_copy(k, k, j, b - k))
        if k == 2 and relay:
            @pl.when(far_side)
            def _():
                act(rel_copy(j))

    def down(j):
        for k in range(2, N, 2):
            @pl.when(b >= k)
            def _():
                duo_add(k, j)
                down_sends(k, j, start)

        @pl.when(even & (b >= N - 1) & not_top)
        def _():
            @pl.when(j >= H)
            def _():
                duo_add(N - 1, j)
            ret_copy(N - 1, N - 1, j, b - (N - 1)).start()

    def relay_down(j):
        remote(rel.at[j], rel.at[j], l_s.at[j], l_r.at[j], b, w).wait_recv()

        def put(value):
            @pl.when(j >= H)
            def _():
                terms[N, j] = (value + terms[N, j].astype(F32)).astype(BF)

            @pl.when(j < H)
            def _():
                terms[N, j] = value.astype(BF)

        @pl.when(even)
        def _():
            put(rel[j].astype(F32))

        @pl.when(odd)
        def _():
            duo_wait(N - 1, j)
            put(rel[j].astype(F32) + duo[N - 1, j].astype(F32))

        ret_copy(N, 2, j, b - N).start()

    def own_back(j):
        own[j] = dot_t(og[0], near[0, col(j), :])
        for k in range(1, N):
            @pl.when(b < k)
            def _():
                own[j] += dot_t(og[k], near[k, col(j), :])

        @pl.when((b < N) & (j < H))
        def _():
            own[j] += dot_t(og[N], far[col(j), :])

    def ret_add(k, j):
        remote(ret.at[k, j], ret.at[k, j], r_s.at[k, j], r_r.at[k, j], b, w).wait_recv()
        own[j] += ret[k, j].astype(F32)

    def collect(j):
        @pl.when(even)
        def _():
            ret_add(1, j)
        for k in range(2, N, 2):
            @pl.when(b + k < B)
            def _():
                ret_add(k, j)

        @pl.when(odd & (b + N - 1 < B) & not_mid)
        def _():
            ret_add(N - 1, j)

        @pl.when(even & (b + N < B) & (j >= H) & not_mid)
        def _():
            ret_add(N, j)

    def finish_back(j):
        def put(value):
            grads = (mask[j].astype(F32) * value).astype(BF)
            pg_ref[:, col(j)] = grads

            @pl.when(w == ROOT)
            def _():
                gb[:, col(j)] = jnp.sum(grads.astype(F32), axis=0, keepdims=True)

        total(1, j, put)

    DUO, RELAY, RING = 3, 6, 10

    def backward(t):
        @pl.when(t < G)
        def _():
            back(t)

        d = t - DUO

        @pl.when(inside(d))
        def _():
            down(d)

        if relay:
            r = t - RELAY

            @pl.when(top & inside(r))
            def _():
                relay_down(r)

        s = t - RING
        for k in range(1, N + 1):
            @pl.when((s == 0) & (b < k))
            def _():
                remote(og.at[k], og.at[k], o_s.at[k], o_r.at[k], b, w).wait_recv()

        @pl.when(inside(s))
        def _():
            own_back(s)
            collect(s)
            ends(1, s)

        hop(1, s)
        f = s - (W - 2)

        @pl.when(inside(f))
        def _():
            finish_back(f)

    loop(0, G + RING + W - 2, backward)

    @pl.when(w == ROOT)
    def _():
        for d in range(1, W):
            bias_copy(d).start()

    def drain(j):
        for phase in range(2):
            @pl.when(w < W - 1)
            def _():
                z_copy(2 * phase, j, w + 1).wait_send()

            @pl.when(w > 0)
            def _():
                z_copy(2 * phase + 1, j, w - 1).wait_send()
        act_sends(j, end)
        for k in list(range(2, N, 2)) + [N - 1]:
            cond = b >= k
            if k == N - 1:
                cond = cond & even & not_top

            @pl.when(cond)
            def _():
                act_forwards(k, j, end)
        if relay:
            @pl.when(top)
            def _():
                relay_sends(j, end)
                ret_copy(N, 2, j, b - N).wait_send()
        for k in range(1, N + 1):
            cond = b >= k
            if k == N:
                cond = cond & (j >= H)

            @pl.when(cond)
            def _():
                duo_sends(k, j, end)
        for k in range(2, N, 2):
            @pl.when(b >= k)
            def _():
                down_sends(k, j, end)

        @pl.when(even & (b >= N - 1) & not_top)
        def _():
            ret_copy(N - 1, N - 1, j, b - (N - 1)).wait_send()

    loop(0, G, drain)
    for k in range(1, N + 1):
        @pl.when(b < k)
        def _():
            share(k).wait_send()

        @pl.when(b + k >= B)
        def _():
            out_grad(k).wait_send()

    @pl.when(w == ROOT)
    def _():
        for d in range(1, W):
            bias_copy(d).wait_send()

    @pl.when(w != ROOT)
    def _():
        bias_copy(1).wait_recv()

    gb_ref[...] = gb[...]


def weight_kernel(x_ref, pg_ref, recon_ref, gb_ref, grad_ref, recon_out, gb_out):
    grad_ref[...] = lax.dot_general(
        x_ref[...], pg_ref[...], (((0,), (0,)), ((), ())), preferred_element_type=F32
    ).astype(BF)
    recon_out[...] = recon_ref[...]
    gb_out[...] = gb_ref[...]


def on_device(B, W, inputs, encoder, enc_bias, active_blocks, near_decoders, far_decoders, targets):
    N = B // 2
    x = inputs[0]
    tok, width = x.shape
    feats = encoder.shape[2]
    half = far_decoders.shape[1]
    out_cols = targets.shape[2]
    C = min(half, 256)
    G = feats // C
    dma = pltpu.SemaphoreType.DMA
    blocks = lambda *lead: pltpu.VMEM((*lead, tok, C), BF)
    rows = lambda *lead: pltpu.VMEM((*lead, tok, out_cols), BF)
    vmem = pl.BlockSpec(memory_space=pltpu.VMEM)
    hbm = pl.BlockSpec(memory_space=pl.ANY)
    recon, pre_grad, bias_sum = pl.pallas_call(
        functools.partial(step_kernel, B, W, C, feats // active_blocks.shape[2]),
        out_shape=(jax.ShapeDtypeStruct((tok, out_cols), F32), jax.ShapeDtypeStruct((tok, feats), BF),
                   jax.ShapeDtypeStruct((1, feats), F32)),
        in_specs=[vmem, hbm, vmem, vmem, hbm, hbm, vmem],
        out_specs=(vmem, vmem, vmem),
        scratch_shapes=[
            pltpu.VMEM((width, feats), BF),
            pltpu.VMEM((N, feats, out_cols), BF),
            pltpu.VMEM((half, out_cols), BF),
            blocks(4, G), blocks(4, G), blocks(N + 1, G),
            pltpu.VMEM((N + 1, tok, out_cols), F32),
            rows(N + 1), rows(N + 1), rows(N + 1),
            blocks(N + 1, G), blocks(N, G), blocks(N + 1, G), blocks(G),
            pltpu.VMEM((G, tok, C), F32),
            blocks(G),
            pltpu.VMEM((1, feats), F32),
            dma((G,)), dma((N,)), dma,
            dma((4, G)), dma((4, G)),
            dma((N + 1, G)), dma((N + 1, G)), dma((N + 1, G)),
            dma((N + 1,)), dma((N + 1,)), dma((N + 1,)), dma((N + 1,)),
            dma((N + 1, G)), dma((N, G)), dma((N + 1, G)), dma((N + 1, G)),
            dma((G,)), dma((G,)), dma((W,)), dma,
        ],
        compiler_params=pltpu.CompilerParams(
            collective_id=0, has_side_effects=True, vmem_limit_bytes=67_000_000),
        name="step",
    )(x, encoder[0], enc_bias, active_blocks[0].T, near_decoders[0], far_decoders[0], targets[0])
    steps = max(1, feats // 1024)
    tile = feats // steps
    part = tok // steps
    enc_grad, recon, bias_grad = pl.pallas_call(
        weight_kernel,
        grid=(steps,),
        out_shape=(jax.ShapeDtypeStruct((width, feats), BF), jax.ShapeDtypeStruct((tok, out_cols), F32),
                   jax.ShapeDtypeStruct((1, feats), F32)),
        in_specs=[pl.BlockSpec((tok, width), lambda i: (0, 0)), pl.BlockSpec((tok, tile), lambda i: (0, i)),
                  pl.BlockSpec((part, out_cols), lambda i: (i, 0)), pl.BlockSpec((1, tile), lambda i: (0, i))],
        out_specs=(pl.BlockSpec((width, tile), lambda i: (0, i)), pl.BlockSpec((part, out_cols), lambda i: (i, 0)),
                   pl.BlockSpec((1, tile), lambda i: (0, i))),
        name="weights",
    )(x, pre_grad, recon, bias_sum)
    return recon[None], enc_grad[None], bias_grad


def solution(mesh):
    return jax.shard_map(
        functools.partial(on_device, mesh.shape["blk"], mesh.shape["width"]),
        mesh=mesh,
        in_specs=(
            P("blk", None, "width"),
            P("blk", "width", None),
            P("blk", None),
            P("blk", None, None),
            P("blk", None, None, "width"),
            P("blk", None, "width"),
            P("blk", None, "width"),
        ),
        out_specs=(P("blk", None, "width"), P("blk", "width", None), P("blk", None)),
        check_vma=False,
    )
```

time: 165 us -> 162 us (0.982)
  the two profiles are of different devices: /device:TPU:16 before, /device:TPU:0 now
where the time goes in v1:
time: 162 us
  Pallas kernels  161 us (99%)
    pallas_call x1, Pallas kernels, on_device(): pl.pallas_call(functools.partial(step_kernel, B, W, C, feats // active_bl...  156 us
    pallas_call x1, Pallas kernels, on_device(): pl.pallas_call(weight_kernel, grid=(steps,), out_shape=(jax.ShapeDtypeStr...  4.94 us

profile of v1, /device:TPU:0, one launch (start us, length us, event | category | flops | bytes accessed | tf_op | source)
XLA Modules:
  0.0 161.9 jit_solution(12960081485233970391)
XLA Ops:
  0.6 156.4 %step.1 = (f32[128,512]{1,0:T(8,128)}, bf16[128,4096]{1,0:T(8,128)(2,1)}, f32[1,4096]{1,0:T(1,128)}) custom-call(bf16[128,512]{1,0:T(8,128)(2,1)} %bitcast.13, bf16[512,4096]{1,0:T(8,128)(2,1)} %bitcast.11, f32[1,4096]{1,0:T(1,128)} %bias_ref.1, s32[32,128]{1,0:T(8,128)} %bitcast.16, bf16[4,4096,512]{2,1,0:T(8,128)(2,1)} %bitcast.10, ...), custom_call_target="tpu_custom_call" | custom-call | tf_op jit(solution)/shard_map/step/pallas_call | solution.py:590
  157.0 4.9 %weights.1 = (bf16[512,4096]{1,0:T(8,128)(2,1)}, f32[128,512]{1,0:T(8,128)}, f32[1,4096]{1,0:T(1,128)}) custom-call(bf16[128,512]{1,0:T(8,128)(2,1)} %bitcast.14, bf16[128,4096]{1,0:T(8,128)(2,1)} %get-tuple-element.9.pg_ref, f32[128,512]{1,0:T(8,128)} %get-tuple-element.10.recon_ref, f32[1,4096]{1,0:T(1,128)} %get-tuple-element.11.gb_ref), custom_call_target="tpu_custom_call" | custom-call | tf_op jit(solution)/shard_map/weights/pallas_call | solution.py:621

commit v2 on v1

--- a/solution.py
+++ b/solution.py
@@ -25,9 +25,12 @@
                 enc_sem, near_sem, far_sem, z_s, z_r, ad_s, af_s, a_r, p_s, p_r, o_s, o_r,
                 d_s, d_r, r_s, r_r, l_s, l_r, g_s, g_r):
     N = B // 2
-    G = mask.shape[0]
+    G = own.shape[0]
     H = G // 2
+    E = G // enc_sem.shape[0]
     ROOT = W // 2
+    SKEW, AHEAD, LATE, BEHIND = 4, 4, 4, 4
+    DUO, RELAY, RING = 3, 6, 10
     b = lax.axis_index("blk")
     w = lax.axis_index("width")
     even = lax.rem(b, 2) == 0
@@ -40,7 +43,7 @@
     not_top = jnp.logical_not(top)
     not_far_side = jnp.logical_not(far_side)
     chip = lax.div(b, 2)
-    late = 2 * (lax.div(chip, 2) - lax.div(chip, 3)) if relay else 0
+    late = LATE * (lax.div(chip, 2) - lax.div(chip, 3)) if relay else 0
 
     def col(j):
         return pl.ds(pl.multiple_of(j * C, C), C)
@@ -59,7 +62,8 @@
         return (j >= 0) & (j < G)
 
     def enc_copy(j):
-        return pltpu.make_async_copy(enc_hbm.at[:, col(j)], enc.at[:, col(j)], enc_sem.at[j])
+        part = pl.ds(pl.multiple_of(j * (E * C), E * C), E * C)
+        return pltpu.make_async_copy(enc_hbm.at[:, part], enc.at[:, part], enc_sem.at[j])
 
     def near_copy(k):
         return pltpu.make_async_copy(near_hbm.at[k], near.at[k], near_sem.at[k])
@@ -67,33 +71,45 @@
     far_copy = pltpu.make_async_copy(far_hbm, far, far_sem)
 
     def z_copy(lane, j, to):
-        return remote(z_out.at[lane, j], z_in.at[lane, j], z_s.at[lane, j], z_r.at[lane, j], b, to)
+        return remote(z_out.at[lane, j], z_in.at[lane, j], z_s.at[lane], z_r.at[lane, j], b, to)
 
     def act_direct(k, j):
-        return remote(acts.at[0, j], acts.at[k, j], ad_s.at[k, j], a_r.at[k, j], b + k, w)
+        return remote(acts.at[0, j], acts.at[k, j], ad_s.at[k], a_r.at[k - 1, j], b + k, w)
 
     def act_pass(k_from, k, j, to):
-        return remote(acts.at[k_from, j], acts.at[k, j], af_s.at[k, j], a_r.at[k, j], to, w)
+        return remote(acts.at[k_from, j], acts.at[k, j], af_s.at[k], a_r.at[k - 1, j], to, w)
 
     def share(k):
         return remote(p_out.at[k], p_in.at[k], p_s.at[k], p_r.at[k], b - k + B, w)
 
+    def share_pair(k):
+        return remote(p_out.at[k], p_in.at[k - 1], p_s.at[k], p_r.at[k - 1], b - 1, w)
+
+    def share_wait(k):
+        remote(p_out.at[k], p_in.at[k], p_s.at[k], p_r.at[k], b, w).wait_recv()
+
     def out_grad(k):
         return remote(og.at[0], og.at[k], o_s.at[k], o_r.at[k], b + k - B, w)
 
+    def grad_pair(k):
+        return remote(og.at[k], og.at[k + 1], o_s.at[k], o_r.at[k + 1], b + 1, w)
+
+    def paired(k):
+        return even if k % 2 == 0 else odd
+
     def duo_copy(k_from, k, j, to):
-        return remote(terms.at[k_from, j], duo.at[k, j], d_s.at[k_from, j], d_r.at[k, j], to, w)
+        return remote(terms.at[k_from, j], duo.at[k - 2, j], d_s.at[k_from], d_r.at[k - 2, j], to, w)
 
     def ret_copy(k_from, k, j, to):
-        return remote(terms.at[k_from, j], ret.at[k, j], r_s.at[k_from, j], r_r.at[k, j], to, w)
+        return remote(terms.at[k_from, j], ret.at[k, j], r_s.at[k_from], r_r.at[k - 1, j], to, w)
 
     def rel_copy(j):
-        return remote(terms.at[2, j], rel.at[j], l_s.at[j], l_r.at[j], b + 2, w)
+        return remote(terms.at[2, j], rel.at[j], l_s, l_r.at[j], b + 2, w)
 
     def bias_copy(d):
         return remote(gb, gb, g_s.at[d], g_r, b, lax.rem(w + d, W))
 
-    loop(0, G, lambda j: enc_copy(j).start())
+    loop(0, G // E, lambda j: enc_copy(j).start())
 
     barrier = pltpu.get_barrier_semaphore()
     for d in range(1, W):
@@ -101,16 +117,12 @@
     for d in range(1, B):
         pl.semaphore_signal(barrier, inc=1, device_id=(lax.rem(b + d, B), w), device_id_type=pl.DeviceIdType.MESH)
 
-    fb = blocks_ref.shape[0]
+    fb, feats = blocks_ref.shape[0], bias_ref.shape[1]
+    row_id = lax.broadcasted_iota(jnp.int32, (fb, feats), 0)
+    lane_id = lax.broadcasted_iota(jnp.int32, (fb, feats), 1) // FBLK
+    spread = jnp.where(row_id == lane_id, 1.0, 0.0).astype(BF)
     active = blocks_ref[...].astype(F32).astype(BF)
-    row_id = lax.broadcasted_iota(jnp.int32, (fb, C), 0)
-    lane_id = lax.broadcasted_iota(jnp.int32, (fb, C), 1) // FBLK
-
-    def masks(j):
-        spread = jnp.where(row_id - j * (C // FBLK) == lane_id, 1.0, 0.0).astype(BF)
-        mask[j] = lax.dot_general(active, spread, (((0,), (0,)), ((), ())), preferred_element_type=F32).astype(BF)
-
-    loop(0, G, masks)
+    mask[...] = lax.dot_general(active, spread, (((0,), (0,)), ((), ())), preferred_element_type=F32).astype(BF)
     recon_ref[...] = jnp.zeros(recon_ref.shape, F32)
     p_acc[...] = jnp.zeros(p_acc.shape, F32)
     pl.semaphore_wait(barrier, W + B - 2)
@@ -127,7 +139,10 @@
             z_copy(2 * phase + 1, j, w - 1).start()
 
     def first(j):
-        enc_copy(j).wait()
+        @pl.when(lax.rem(j, E) == 0)
+        def _():
+            enc_copy(lax.div(j, E)).wait()
+
         own[j] = dot(x_ref[...], enc[:, col(j)])
         ends(0, j)
 
@@ -137,8 +152,8 @@
     far_copy.start()
 
     def hop(phase, t):
-        up = t - w + 1
-        down = t - (W - 2) + w
+        up = t - SKEW * (w - 1)
+        down = t - SKEW * (W - 2 - w)
 
         @pl.when((w > 0) & inside(up))
         def _():
@@ -190,11 +205,10 @@
             act(act_direct(N, j))
 
     start = lambda c: c.start()
-    end = lambda c: c.wait_send()
 
     def finish(j):
         def put(value):
-            acts[0, j] = (mask[j].astype(F32) * (value + bias_ref[:, col(j)])).astype(BF)
+            acts[0, j] = (mask[:, col(j)].astype(F32) * (value + bias_ref[:, col(j)])).astype(BF)
 
         total(0, j, put)
         act_sends(j, start)
@@ -229,7 +243,7 @@
                 act(act_pass(k, N, j, b + 1))
 
     def arrival(k, j):
-        return remote(acts.at[k, j], acts.at[k, j], ad_s.at[k, j], a_r.at[k, j], b, w)
+        return remote(acts.at[k, j], acts.at[k, j], ad_s.at[k], a_r.at[k - 1, j], b, w)
 
     def relay_sends(j, act):
         act(act_pass(N, 2, j, b - 2))
@@ -276,11 +290,10 @@
                 arrival(k, j).wait_recv()
                 inside_term(k, j)
 
-    AHEAD, BEHIND = 3, 3
 
     def forward(t):
         hop(0, t)
-        f = t - (W - 2)
+        f = t - SKEW * (W - 2)
 
         @pl.when(f == 0)
         def _():
@@ -293,8 +306,17 @@
             finish(f)
 
         for k in range(1, N + 1):
-            @pl.when((f == G - 1) & (b < k))
-            def _():
+            if k > 1:
+                @pl.when((f == G - 1) & (b < k) & odd)
+                def _():
+                    p_out[k] = p_acc[k].astype(BF)
+                    share_pair(k).start()
+
+            @pl.when((f == G + 1) & (b < k) & even)
+            def _():
+                if k < N:
+                    share_wait(k)
+                    p_acc[k] += p_in[k].astype(F32)
                 p_out[k] = p_acc[k].astype(BF)
                 share(k).start()
 
@@ -310,16 +332,16 @@
         def _():
             passed(p)
 
-    loop(0, G + W - 2 + AHEAD + BEHIND + (2 if relay else 0), forward)
+    loop(0, G + SKEW * (W - 2) + AHEAD + BEHIND + (LATE if relay else 0), forward)
     for k in range(1, N + 1):
-        @pl.when(b + k >= B)
-        def _():
-            remote(p_out.at[k], p_in.at[k], p_s.at[k], p_r.at[k], b, w).wait_recv()
+        @pl.when((b + k >= B) & paired(k))
+        def _():
+            share_wait(k)
             recon_ref[...] += p_in[k].astype(F32)
 
     og[0] = (recon_ref[...] - tgt_ref[...].astype(F32)).astype(BF)
     for k in range(1, N + 1):
-        @pl.when(b + k >= B)
+        @pl.when((b + k >= B) & paired(k))
         def _():
             out_grad(k).start()
 
@@ -362,11 +384,11 @@
                 act(ret_copy(N, N, j, b - N))
 
     def duo_wait(k, j):
-        remote(duo.at[k, j], duo.at[k, j], d_s.at[k, j], d_r.at[k, j], b, w).wait_recv()
+        remote(duo.at[k - 2, j], duo.at[k - 2, j], d_s.at[k], d_r.at[k - 2, j], b, w).wait_recv()
 
     def duo_add(k, j):
         duo_wait(k, j)
-        terms[k, j] = (terms[k, j].astype(F32) + duo[k, j].astype(F32)).astype(BF)
+        terms[k, j] = (terms[k, j].astype(F32) + duo[k - 2, j].astype(F32)).astype(BF)
 
     def down_sends(k, j, act):
         @pl.when(not_far_side)
@@ -392,7 +414,7 @@
             ret_copy(N - 1, N - 1, j, b - (N - 1)).start()
 
     def relay_down(j):
-        remote(rel.at[j], rel.at[j], l_s.at[j], l_r.at[j], b, w).wait_recv()
+        remote(rel.at[j], rel.at[j], l_s, l_r.at[j], b, w).wait_recv()
 
         def put(value):
             @pl.when(j >= H)
@@ -410,7 +432,7 @@
         @pl.when(odd)
         def _():
             duo_wait(N - 1, j)
-            put(rel[j].astype(F32) + duo[N - 1, j].astype(F32))
+            put(rel[j].astype(F32) + duo[N - 3, j].astype(F32))
 
         ret_copy(N, 2, j, b - N).start()
 
@@ -426,7 +448,7 @@
             own[j] += dot_t(og[N], far[col(j), :])
 
     def ret_add(k, j):
-        remote(ret.at[k, j], ret.at[k, j], r_s.at[k, j], r_r.at[k, j], b, w).wait_recv()
+        remote(ret.at[k, j], ret.at[k, j], r_s.at[k], r_r.at[k - 1, j], b, w).wait_recv()
         own[j] += ret[k, j].astype(F32)
 
     def collect(j):
@@ -448,7 +470,7 @@
 
     def finish_back(j):
         def put(value):
-            grads = (mask[j].astype(F32) * value).astype(BF)
+            grads = (mask[:, col(j)].astype(F32) * value).astype(BF)
             pg_ref[:, col(j)] = grads
 
             @pl.when(w == ROOT)
@@ -457,7 +479,6 @@
 
         total(1, j, put)
 
-    DUO, RELAY, RING = 3, 6, 10
 
     def backward(t):
         @pl.when(t < G)
@@ -482,6 +503,10 @@
             @pl.when((s == 0) & (b < k))
             def _():
                 remote(og.at[k], og.at[k], o_s.at[k], o_r.at[k], b, w).wait_recv()
+                if k < N:
+                    @pl.when(even)
+                    def _():
+                        grad_pair(k).start()
 
         @pl.when(inside(s))
         def _():
@@ -490,66 +515,66 @@
             ends(1, s)
 
         hop(1, s)
-        f = s - (W - 2)
+        f = s - SKEW * (W - 2)
 
         @pl.when(inside(f))
         def _():
             finish_back(f)
 
-    loop(0, G + RING + W - 2, backward)
+    loop(0, G + RING + SKEW * (W - 2), backward)
 
     @pl.when(w == ROOT)
     def _():
         for d in range(1, W):
             bias_copy(d).start()
 
-    def drain(j):
-        for phase in range(2):
-            @pl.when(w < W - 1)
-            def _():
-                z_copy(2 * phase, j, w + 1).wait_send()
-
-            @pl.when(w > 0)
-            def _():
-                z_copy(2 * phase + 1, j, w - 1).wait_send()
-        act_sends(j, end)
-        for k in list(range(2, N, 2)) + [N - 1]:
-            cond = b >= k
-            if k == N - 1:
-                cond = cond & even & not_top
-
-            @pl.when(cond)
-            def _():
-                act_forwards(k, j, end)
-        if relay:
-            @pl.when(top)
-            def _():
-                relay_sends(j, end)
-                ret_copy(N, 2, j, b - N).wait_send()
-        for k in range(1, N + 1):
-            cond = b >= k
-            if k == N:
-                cond = cond & (j >= H)
-
-            @pl.when(cond)
-            def _():
-                duo_sends(k, j, end)
-        for k in range(2, N, 2):
-            @pl.when(b >= k)
-            def _():
-                down_sends(k, j, end)
-
-        @pl.when(even & (b >= N - 1) & not_top)
-        def _():
-            ret_copy(N - 1, N - 1, j, b - (N - 1)).wait_send()
-
-    loop(0, G, drain)
+    def sent(buf, k, n, sem, cond):
+        @pl.when(cond)
+        def _():
+            part = buf.at[k, pl.ds(0, n)]
+            remote(part, part, sem, sem, b, w).wait_send()
+
+    for phase in range(2):
+        sent(z_out, 2 * phase, G, z_s.at[2 * phase], w < W - 1)
+        sent(z_out, 2 * phase + 1, G, z_s.at[2 * phase + 1], w > 0)
+    sent(acts, 0, G, af_s.at[1], even)
+    for k in range(2, N, 2):
+        sent(acts, 0, G, ad_s.at[k], (b + k < B) & not_mid)
+        sent(acts, k, G, af_s.at[k + 1], even & (b >= k))
+        sent(acts, k, G, af_s.at[k - 1], odd & (b >= k))
+    sent(acts, 0, G, ad_s.at[N - 1], odd & (b + N - 1 < B) & not_mid)
+    sent(acts, 0, H, ad_s.at[N], even & (b + N < B) & not_mid)
+    sent(acts, N - 1, H, af_s.at[N], even & (b >= N - 1) & not_top)
+    for k in range(1, N, 2):
+        if k <= N - 3:
+            sent(terms, k, G, d_s.at[k], even & (b >= k))
+        if k >= 3:
+            sent(terms, k, G, d_s.at[k], odd & (b >= k))
+    sent(terms, 1, G, r_s.at[1], odd)
+    sent(terms, N, H, d_s.at[N], odd & (b >= N) & not_top)
+    sent(terms, N, H, r_s.at[N], even & (b >= N) & not_top)
+    for k in range(2, N, 2):
+        sent(terms, k, G, r_s.at[k], (b >= k) & not_far_side if k == 2 else b >= k)
+    sent(terms, N - 1, G, r_s.at[N - 1], even & (b >= N - 1) & not_top)
+    if relay:
+        sent(acts, 0, G, ad_s.at[N], mid)
+        sent(acts, N, G, af_s.at[2], top)
+        sent(acts, N, G, af_s.at[N - 1], top & odd)
+        sent(terms, N - 1, G, d_s.at[N - 1], top & even)
+        sent(terms, 2, G, l_s, far_side)
+        sent(terms, N, G, r_s.at[N], top)
     for k in range(1, N + 1):
-        @pl.when(b < k)
+        @pl.when((b < k) & even)
         def _():
             share(k).wait_send()
-
-        @pl.when(b + k >= B)
+            if k < N:
+                grad_pair(k).wait_send()
+        if k > 1:
+            @pl.when((b < k) & odd)
+            def _():
+                share_pair(k).wait_send()
+
+        @pl.when((b + k >= B) & paired(k))
         def _():
             out_grad(k).wait_send()
 
@@ -600,16 +625,16 @@
             blocks(4, G), blocks(4, G), blocks(N + 1, G),
             pltpu.VMEM((N + 1, tok, out_cols), F32),
             rows(N + 1), rows(N + 1), rows(N + 1),
-            blocks(N + 1, G), blocks(N, G), blocks(N + 1, G), blocks(G),
+            blocks(N + 1, G), blocks(N - 2, G), blocks(N + 1, G), blocks(G),
             pltpu.VMEM((G, tok, C), F32),
-            blocks(G),
+            pltpu.VMEM((tok, feats), BF),
             pltpu.VMEM((1, feats), F32),
-            dma((G,)), dma((N,)), dma,
-            dma((4, G)), dma((4, G)),
-            dma((N + 1, G)), dma((N + 1, G)), dma((N + 1, G)),
+            dma((min(G, 4),)), dma((N,)), dma,
+            dma((4,)), dma((4, G)),
+            dma((N + 1,)), dma((N + 1,)), dma((N, G)),
             dma((N + 1,)), dma((N + 1,)), dma((N + 1,)), dma((N + 1,)),
-            dma((N + 1, G)), dma((N, G)), dma((N + 1, G)), dma((N + 1, G)),
-            dma((G,)), dma((G,)), dma((W,)), dma,
+            dma((N + 1,)), dma((N - 2, G)), dma((N + 1,)), dma((N, G)),
+            dma, dma((G,)), dma((W,)), dma,
         ],
         compiler_params=pltpu.CompilerParams(
             collective_id=0, has_side_effects=True, vmem_limit_bytes=67_000_000),

time: 162 us -> 106 us (0.65)
  the two profiles are of different devices: /device:TPU:0 before, /device:TPU:6 now
where the time goes in v2:
time: 106 us
  Pallas kernels  105 us (99%)
    pallas_call x1, Pallas kernels, on_device(): pl.pallas_call(functools.partial(step_kernel, B, W, C, feats // active_bl...  100 us
    pallas_call x1, Pallas kernels, on_device(): pl.pallas_call(weight_kernel, grid=(steps,), out_shape=(jax.ShapeDtypeStr...  4.94 us

profile of v2, /device:TPU:6, one launch (start us, length us, event | category | flops | bytes accessed | tf_op | source)
XLA Modules:
  0.0 105.8 jit_solution(4551284865588327985)
XLA Ops:
  0.6 100.2 %step.1 = (f32[128,512]{1,0:T(8,128)}, bf16[128,4096]{1,0:T(8,128)(2,1)}, f32[1,4096]{1,0:T(1,128)}) custom-call(bf16[128,512]{1,0:T(8,128)(2,1)} %bitcast.13, bf16[512,4096]{1,0:T(8,128)(2,1)} %bitcast.11, f32[1,4096]{1,0:T(1,128)} %bias_ref.1, s32[32,128]{1,0:T(8,128)} %bitcast.16, bf16[4,4096,512]{2,1,0:T(8,128)(2,1)} %bitcast.10, ...), custom_call_target="tpu_custom_call" | custom-call | tf_op jit(solution)/shard_map/step/pallas_call | solution.py:615
  100.9 4.9 %weights.1 = (bf16[512,4096]{1,0:T(8,128)(2,1)}, f32[128,512]{1,0:T(8,128)}, f32[1,4096]{1,0:T(1,128)}) custom-call(bf16[128,512]{1,0:T(8,128)(2,1)} %bitcast.14, bf16[128,4096]{1,0:T(8,128)(2,1)} %get-tuple-element.9.pg_ref, f32[128,512]{1,0:T(8,128)} %get-tuple-element.10.recon_ref, f32[1,4096]{1,0:T(1,128)} %get-tuple-element.11.gb_ref), custom_call_target="tpu_custom_call" | custom-call | tf_op jit(solution)/shard_map/weights/pallas_call | solution.py:646

commit v3 on v2

--- a/solution.py
+++ b/solution.py
@@ -29,8 +29,8 @@
     H = G // 2
     E = G // enc_sem.shape[0]
     ROOT = W // 2
-    SKEW, AHEAD, LATE, BEHIND = 4, 4, 4, 4
-    DUO, RELAY, RING = 3, 6, 10
+    SKEW, AHEAD, LATE, EARLY, BEHIND = 4, 4, 2, 2, 4
+    DUO, RELAY, RING = 2, 5, 8
     b = lax.axis_index("blk")
     w = lax.axis_index("width")
     even = lax.rem(b, 2) == 0
@@ -43,7 +43,13 @@
     not_top = jnp.logical_not(top)
     not_far_side = jnp.logical_not(far_side)
     chip = lax.div(b, 2)
-    late = LATE * (lax.div(chip, 2) - lax.div(chip, 3)) if relay else 0
+    on_far_side = lax.div(chip, 2) - lax.div(chip, 3)
+    on_top = lax.div(chip, 3)
+    late = LATE * on_far_side - EARLY * on_top if relay else 0
+    D = G // 4
+    ring = RING - 2 * on_far_side - 4 * on_top if relay else RING
+    upper = lax.div(2 * w, W)
+    fill = SKEW * (upper * (w - 1) + (1 - upper) * (W - 2 - w))
 
     def col(j):
         return pl.ds(pl.multiple_of(j * C, C), C)
@@ -188,7 +194,7 @@
 
     def act_sends(j, act):
         for k in range(2, N, 2):
-            @pl.when((b + k < B) & not_mid)
+            @pl.when((b + k < B) & (not_mid | (j < D)))
             def _():
                 act(act_direct(k, j))
 
@@ -246,7 +252,9 @@
         return remote(acts.at[k, j], acts.at[k, j], ad_s.at[k], a_r.at[k - 1, j], b, w)
 
     def relay_sends(j, act):
-        act(act_pass(N, 2, j, b - 2))
+        @pl.when(j >= D)
+        def _():
+            act(act_pass(N, 2, j, b - 2))
 
         @pl.when(odd)
         def _():
@@ -293,7 +301,7 @@
 
     def forward(t):
         hop(0, t)
-        f = t - SKEW * (W - 2)
+        f = t - fill
 
         @pl.when(f == 0)
         def _():
@@ -498,7 +506,7 @@
             def _():
                 relay_down(r)
 
-        s = t - RING
+        s = t - ring
         for k in range(1, N + 1):
             @pl.when((s == 0) & (b < k))
             def _():
@@ -558,7 +566,8 @@
     sent(terms, N - 1, G, r_s.at[N - 1], even & (b >= N - 1) & not_top)
     if relay:
         sent(acts, 0, G, ad_s.at[N], mid)
-        sent(acts, N, G, af_s.at[2], top)
+        sent(acts, 0, D, ad_s.at[2], mid)
+        sent(acts, N, G - D, af_s.at[2], top)
         sent(acts, N, G, af_s.at[N - 1], top & odd)
         sent(terms, N - 1, G, d_s.at[N - 1], top & even)
         sent(terms, 2, G, l_s, far_side)
@@ -640,7 +649,7 @@
             collective_id=0, has_side_effects=True, vmem_limit_bytes=67_000_000),
         name="step",
     )(x, encoder[0], enc_bias, active_blocks[0].T, near_decoders[0], far_decoders[0], targets[0])
-    steps = max(1, feats // 1024)
+    steps = max(1, feats // 2048)
     tile = feats // steps
     part = tok // steps
     enc_grad, recon, bias_grad = pl.pallas_call(

time: 106 us -> 102 us (0.962)
  the two profiles are of different devices: /device:TPU:6 before, /device:TPU:0 now
where the time goes in v3:
time: 102 us
  Pallas kernels  101 us (99%)
    pallas_call x1, Pallas kernels, on_device(): pl.pallas_call(functools.partial(step_kernel, B, W, C, feats // active_bl...  96.9 us
    pallas_call x1, Pallas kernels, on_device(): pl.pallas_call(weight_kernel, grid=(steps,), out_shape=(jax.ShapeDtypeStr...  4.03 us

profile of v3, /device:TPU:0, one launch (start us, length us, event | category | flops | bytes accessed | tf_op | source)
XLA Modules:
  0.0 101.6 jit_solution(12468832358330516703)
XLA Ops:
  0.6 96.9 %step.1 = (f32[128,512]{1,0:T(8,128)}, bf16[128,4096]{1,0:T(8,128)(2,1)}, f32[1,4096]{1,0:T(1,128)}) custom-call(bf16[128,512]{1,0:T(8,128)(2,1)} %bitcast.13, bf16[512,4096]{1,0:T(8,128)(2,1)} %bitcast.11, f32[1,4096]{1,0:T(1,128)} %bias_ref.1, s32[32,128]{1,0:T(8,128)} %bitcast.16, bf16[4,4096,512]{2,1,0:T(8,128)(2,1)} %bitcast.10, ...), custom_call_target="tpu_custom_call" | custom-call | tf_op jit(solution)/shard_map/step/pallas_call | solution.py:624
  97.5 4.0 %weights.1 = (bf16[512,4096]{1,0:T(8,128)(2,1)}, f32[128,512]{1,0:T(8,128)}, f32[1,4096]{1,0:T(1,128)}) custom-call(bf16[128,512]{1,0:T(8,128)(2,1)} %bitcast.14, bf16[128,4096]{1,0:T(8,128)(2,1)} %get-tuple-element.9.pg_ref, f32[128,512]{1,0:T(8,128)} %get-tuple-element.10.recon_ref, f32[1,4096]{1,0:T(1,128)} %get-tuple-element.11.gb_ref), custom_call_target="tpu_custom_call" | custom-call | tf_op jit(solution)/shard_map/weights/pallas_call | solution.py:655

commit v4 on v3

--- a/solution.py
+++ b/solution.py
@@ -19,17 +19,17 @@
     return lax.dot_general(a, b, (((1,), (1,)), ((), ())), preferred_element_type=F32)
 
 
-def step_kernel(B, W, C, FBLK, x_ref, enc_hbm, bias_ref, blocks_ref, near_hbm, far_hbm, tgt_ref,
+def step_kernel(B, W, C, FBLK, x_hbm, enc_hbm, bias_hbm, blocks_hbm, near_hbm, far_hbm, tgt_hbm,
                 recon_ref, pg_ref, gb_ref,
-                enc, near, far, z_out, z_in, acts, p_acc, p_out, p_in, og, terms, duo, ret, rel, own, mask, gb,
-                enc_sem, near_sem, far_sem, z_s, z_r, ad_s, af_s, a_r, p_s, p_r, o_s, o_r,
+                x_ref, bias_ref, blocks_ref, tgt_ref, enc, near, far, z_out, z_in, acts, p_acc, p_out, p_in, og, terms, duo, ret, rel, own, mask, gb,
+                in_sem, enc_sem, near_sem, far_sem, z_s, z_r, ad_s, af_s, a_r, p_s, p_r, o_s, o_r,
                 d_s, d_r, r_s, r_r, l_s, l_r, g_s, g_r):
     N = B // 2
     G = own.shape[0]
     H = G // 2
     E = G // enc_sem.shape[0]
     ROOT = W // 2
-    SKEW, AHEAD, LATE, EARLY, BEHIND = 4, 4, 2, 2, 4
+    SKEW, AHEAD, LATE, EARLY, BEHIND = 4, 4, 2, 2, 2
     DUO, RELAY, RING = 2, 5, 8
     b = lax.axis_index("blk")
     w = lax.axis_index("width")
@@ -75,6 +75,8 @@
         return pltpu.make_async_copy(near_hbm.at[k], near.at[k], near_sem.at[k])
 
     far_copy = pltpu.make_async_copy(far_hbm, far, far_sem)
+    pairs = ((blocks_hbm, blocks_ref), (x_hbm, x_ref), (bias_hbm, bias_ref), (tgt_hbm, tgt_ref))
+    loads = [pltpu.make_async_copy(src, dst, in_sem.at[i]) for i, (src, dst) in enumerate(pairs)]
 
     def z_copy(lane, j, to):
         return remote(z_out.at[lane, j], z_in.at[lane, j], z_s.at[lane], z_r.at[lane, j], b, to)
@@ -114,8 +116,6 @@
 
     def bias_copy(d):
         return remote(gb, gb, g_s.at[d], g_r, b, lax.rem(w + d, W))
-
-    loop(0, G // E, lambda j: enc_copy(j).start())
 
     barrier = pltpu.get_barrier_semaphore()
     for d in range(1, W):
@@ -123,14 +123,20 @@
     for d in range(1, B):
         pl.semaphore_signal(barrier, inc=1, device_id=(lax.rem(b + d, B), w), device_id_type=pl.DeviceIdType.MESH)
 
+    for load in loads:
+        load.start()
+    loop(0, G // E, lambda j: enc_copy(j).start())
     fb, feats = blocks_ref.shape[0], bias_ref.shape[1]
     row_id = lax.broadcasted_iota(jnp.int32, (fb, feats), 0)
     lane_id = lax.broadcasted_iota(jnp.int32, (fb, feats), 1) // FBLK
     spread = jnp.where(row_id == lane_id, 1.0, 0.0).astype(BF)
+    loads[0].wait()
     active = blocks_ref[...].astype(F32).astype(BF)
     mask[...] = lax.dot_general(active, spread, (((0,), (0,)), ((), ())), preferred_element_type=F32).astype(BF)
     recon_ref[...] = jnp.zeros(recon_ref.shape, F32)
     p_acc[...] = jnp.zeros(p_acc.shape, F32)
+    for load in loads[1:]:
+        load.wait()
     pl.semaphore_wait(barrier, W + B - 2)
 
     def ends(phase, j):
@@ -625,9 +631,13 @@
         functools.partial(step_kernel, B, W, C, feats // active_blocks.shape[2]),
         out_shape=(jax.ShapeDtypeStruct((tok, out_cols), F32), jax.ShapeDtypeStruct((tok, feats), BF),
                    jax.ShapeDtypeStruct((1, feats), F32)),
-        in_specs=[vmem, hbm, vmem, vmem, hbm, hbm, vmem],
+        in_specs=[hbm] * 7,
         out_specs=(vmem, vmem, vmem),
         scratch_shapes=[
+            pltpu.VMEM((tok, width), BF),
+            pltpu.VMEM((1, feats), F32),
+            pltpu.VMEM((active_blocks.shape[2], tok), active_blocks.dtype),
+            pltpu.VMEM((tok, out_cols), BF),
             pltpu.VMEM((width, feats), BF),
             pltpu.VMEM((N, feats, out_cols), BF),
             pltpu.VMEM((half, out_cols), BF),
@@ -638,7 +648,7 @@
             pltpu.VMEM((G, tok, C), F32),
             pltpu.VMEM((tok, feats), BF),
             pltpu.VMEM((1, feats), F32),
-            dma((min(G, 4),)), dma((N,)), dma,
+            dma((4,)), dma((min(G, 4),)), dma((N,)), dma,
             dma((4,)), dma((4, G)),
             dma((N + 1,)), dma((N + 1,)), dma((N, G)),
             dma((N + 1,)), dma((N + 1,)), dma((N + 1,)), dma((N + 1,)),

time: 102 us -> 101 us (level)
  no operation moved by 1% of the time
where the time goes in v4:
time: 101 us
  Pallas kernels  100 us (99%)
    pallas_call x1, Pallas kernels, on_device(): pl.pallas_call(functools.partial(step_kernel, B, W, C, feats // active_bl...  96.1 us
    pallas_call x1, Pallas kernels, on_device(): pl.pallas_call(weight_kernel, grid=(steps,), out_shape=(jax.ShapeDtypeStr...  4.02 us

profile of v4, /device:TPU:0, one launch (start us, length us, event | category | flops | bytes accessed | tf_op | source)
XLA Modules:
  0.0 100.8 jit_solution(4570820252233942680)
XLA Ops:
  0.6 96.1 %step.1 = (f32[128,512]{1,0:T(8,128)}, bf16[128,4096]{1,0:T(8,128)(2,1)}, f32[1,4096]{1,0:T(1,128)}) custom-call(bf16[128,512]{1,0:T(8,128)(2,1)} %bitcast.13, bf16[512,4096]{1,0:T(8,128)(2,1)} %bitcast.11, f32[1,4096]{1,0:T(1,128)} %bias_hbm.1, s32[32,128]{1,0:T(8,128)} %bitcast.16, bf16[4,4096,512]{2,1,0:T(8,128)(2,1)} %bitcast.10, ...), custom_call_target="tpu_custom_call" | custom-call | tf_op jit(solution)/shard_map/step/pallas_call | solution.py:630
  96.8 4.0 %weights.1 = (bf16[512,4096]{1,0:T(8,128)(2,1)}, f32[128,512]{1,0:T(8,128)}, f32[1,4096]{1,0:T(1,128)}) custom-call(bf16[128,512]{1,0:T(8,128)(2,1)} %bitcast.14, bf16[128,4096]{1,0:T(8,128)(2,1)} %get-tuple-element.9.pg_ref, f32[128,512]{1,0:T(8,128)} %get-tuple-element.10.recon_ref, f32[1,4096]{1,0:T(1,128)} %get-tuple-element.11.gb_ref), custom_call_target="tpu_custom_call" | custom-call | tf_op jit(solution)/shard_map/weights/pallas_call | solution.py:665
